TPU v7x, 32 devices: a whole 2x2x4 slice. The times are simulated.
32 devices in a mesh: mem: 2 (over y), lat: 4 (over z), lon: 4 (over x, core).
Axes of the slice: x: 2, y: 2, z: 4, core: 2. Of those that a mesh axis runs over, the one named last changes fastest.
Arguments:
- control: bfloat16 [62, 3, 4, 4, 73728], P('mem', None, 'lat', 'lon'), may hold values from -6 to 6
- perturbs: bfloat16 [62, 3, 4, 4, 73728], P('mem', None, 'lat', 'lon'), may hold values from -0.75 to 0.75
- static_input: bfloat16 [3, 4, 4, 73728], P(None, 'lat', 'lon'), may hold values from -6 to 6
- lat_basis: bfloat16 [768, 384], replicated, may hold values from -0.21875 to 0.21875
- local_spectrum: float32 [384, 768], P(None, 'lat'), may hold values from 0.1 to 1
- static_spectrum: float32 [384, 768], P(None, 'lat'), may hold values from 0.1 to 1
- static_weight: float32 [3], replicated, may hold values from 0.2 to 0.8
Outputs:
- increment: float32 [3, 4, 4, 73728], P(None, 'lat', 'lon')
All inputs are finite; a program needn't handle non-finite values.
Results may differ from a plain program's by a relative error of at most 0.0073.
Values may be sent and summed in bfloat16 or wider, within the bound.
A program may use at most 128 MiB of HBM per device.

v0:
```python
import jax
import jax.numpy as jnp
from jax import lax
from jax.sharding import PartitionSpec as P

NLON = 1536
NLAT = 768
KLON = 768


def zonal_table():
    half = KLON // 2
    points = jnp.arange(NLON, dtype=jnp.int32)
    column = jnp.arange(KLON, dtype=jnp.int32)
    wave = jnp.where(column < half, column, column - half + 1)
    phase = points[:, None] * wave[None, :] % NLON
    angle = 2.0 * jnp.pi / NLON * phase.astype(jnp.float32)
    scale = jnp.sqrt(jnp.float32(2.0 / NLON))
    values = jnp.where(column[None, :] < half, jnp.cos(angle), jnp.sin(angle)) * scale
    return values.astype(jnp.bfloat16)


def shards(
    control, perturbs, static_input, lat_basis, local_spectrum, static_spectrum, static_weight
):
    mem_dev, levels = (control.shape[0], control.shape[1])
    cell_count = control.shape[-1]
    lat_rows = NLAT // lax.axis_size("lat")
    lon_cols = cell_count // lat_rows
    fields = jnp.concatenate([control, static_input[None]], 0).reshape(-1, lat_rows, lon_cols)
    per_lon = fields.shape[0] // lax.axis_size("lon")
    field_index = lax.axis_index("lon") * per_lon + jnp.arange(per_lon, dtype=jnp.int32)
    is_static = field_index >= mem_dev * levels
    first_mem = (lax.axis_index("mem") == 0).astype(jnp.float32)
    zonal = zonal_table()
    strips = lax.all_to_all(fields, "lon", split_axis=0, concat_axis=2, tiled=True)
    waves = jnp.einsum("bxn,nk->kbx", strips, zonal, preferred_element_type=jnp.float32).astype(
        jnp.bfloat16
    )
    merid = lax.all_to_all(waves, "lat", split_axis=0, concat_axis=2, tiled=True)
    coef = jnp.einsum("kby,yj->kbj", merid, lat_basis, preferred_element_type=jnp.float32)
    spectrum = jnp.where(
        is_static[None, :, None], static_spectrum.T[:, None, :], local_spectrum.T[:, None, :]
    )
    scaled = (coef * spectrum).astype(jnp.bfloat16)
    back = jnp.einsum("kbj,yj->kby", scaled, lat_basis, preferred_element_type=jnp.float32).astype(
        jnp.bfloat16
    )
    zonal_rows = lax.all_to_all(back, "lat", split_axis=2, concat_axis=0, tiled=True)
    grid = jnp.einsum("kbx,nk->bxn", zonal_rows, zonal, preferred_element_type=jnp.float32).astype(
        jnp.bfloat16
    )
    pert_fields = perturbs.reshape(mem_dev, levels, lat_rows, lon_cols)
    weight = static_weight[:, None, None]
    filtered = lax.all_to_all(grid, "lon", split_axis=2, concat_axis=0, tiled=True).reshape(
        mem_dev + 1, levels, lat_rows, lon_cols
    )
    ensemble = jnp.einsum(
        "mlxn,mlxn->lxn", pert_fields, filtered[:mem_dev], preferred_element_type=jnp.float32
    )
    static_part = filtered[mem_dev].astype(jnp.float32)
    own = first_mem * weight * static_part + (1.0 - weight) * ensemble
    total = lax.psum(own, "mem")
    return total.reshape(levels, 1, 1, cell_count)


def solution(mesh):
    return jax.shard_map(
        shards,
        mesh=mesh,
        in_specs=(
            P("mem", None, "lat", "lon", None),
            P("mem", None, "lat", "lon", None),
            P(None, "lat", "lon", None),
            P(),
            P(None, "lat"),
            P(None, "lat"),
            P(),
        ),
        out_specs=P(None, "lat", "lon", None),
        check_vma=False,
    )
```

profile of v0, /device:TPU:0, one launch (start us, length us, event | category | flops | bytes accessed | tf_op | source)
XLA Modules:
  0.0 1161.2 jit_solution(15015766370873050855)
XLA Ops:
  6.5 1.9 copy.44
  8.4 8.6 pad_maximum_fusion
  17.1 48.5 %copy.45 = bf16[32,3,1,1,73728]{4,1,0,3,2:T(4,128)(2,1)} copy(bf16[32,3,1,1,73728]{4,0,3,2,1:T(8,128)(2,1)S(1)} %pad_maximum_fusion) | data formatting | bytes 28311552 | tf_op jit(solution)/shard_map/concatenate | solution.py:30
  65.6 31.2 %reshape.38 = bf16[96,192,384]{2,1,0:T(8,128)(2,1)} reshape(bf16[32,3,1,1,73728]{4,1,0,3,2:T(4,128)(2,1)} %copy.45) | data formatting | bytes 28311552 | tf_op jit(solution)/shard_map/reshape | solution.py:30
  96.8 6.8 all-to-all-start
  103.7 19.8 %fusion.43 = bf16[1536,768,1]{1,0,2:T(8,128)(2,1)S(1)} fusion(s32[768]{0:T(1024)S(1)} %add_select_fusion.1, pred[768]{0:T(1024)(128)(4,1)S(1)} %iota_compare_fusion), kind=kLoop, calls=%fused_computation.21.clone.1.clone.1 | loop fusion | flops 14155776 | bytes 2363136 | tf_op jit(solution)/shard_map/bxn,nk->kbx/dot_general | solution.py:37
  123.5 135.9 %all-to-all-done = bf16[96,192,384]{2,1,0:T(8,128)(2,1)} async-done(((bf16[96,192,384]{2,1,0:T(8,128)(2,1)}), bf16[96,192,384]{2,1,0:T(8,128)(2,1)}, u32[]{:S(2)}, u32[]{:S(2)}) %all-to-all-start) | async-done | bytes 14155808 | tf_op jit(solution)/shard_map/all_to_all | solution.py:36
  259.4 10.6 copy.62
  270.0 16.3 %convolution_convert_fusion.2 = bf16[768,24,192]{0,2,1:T(8,128)(2,1)} fusion(bf16[24,192,1536]{2,1,0:T(8,128)(2,1)} %bitcast.63, bf16[1536,768,1]{1,0,2:T(8,128)(2,1)S(1)} %fusion.43), kind=kOutput, calls=%fused_computation.10 | convolution fusion | flops 10875174912 | bytes 23592960 | tf_op jit(solution)/shard_map/bxn,nk->kbx/dot_general | solution.py:37
  286.3 13.4 %copy.47 = bf16[768,24,192]{2,1,0:T(8,128)(2,1)} copy(bf16[768,24,192]{0,2,1:T(8,128)(2,1)} %convolution_convert_fusion.2) | data formatting | bytes 14155776 | tf_op jit(solution)/shard_map/convert_element_type | solution.py:37
  299.7 6.3 all-to-all-start.1
  306.1 206.2 %all-to-all-done.1 = bf16[768,24,192]{2,1,0:T(8,128)(2,1)} async-done(((bf16[768,24,192]{2,1,0:T(8,128)(2,1)}), bf16[768,24,192]{2,1,0:T(8,128)(2,1)}, u32[]{:S(2)}, u32[]{:S(2)}) %all-to-all-start.1) | async-done | bytes 7077920 | tf_op jit(solution)/shard_map/all_to_all | solution.py:40
  512.2 20.1 %copy.67 = bf16[4,192,24,192]{3,0,2,1:T(4,128)(2,1)} copy(bf16[4,192,24,192]{3,2,1,0:T(8,128)(2,1)} %bitcast.6) | data formatting | bytes 14155776 | tf_op jit(solution)/shard_map/all_to_all | solution.py:40
  532.3 16.6 %all_to_all.57 = bf16[192,24,768]{2,1,0:T(8,128)(2,1)} reshape(bf16[192,24,4,192]{3,2,1,0:T(4,128)(2,1)} %bitcast.61) | data formatting | bytes 14155776 | tf_op jit(solution)/shard_map/all_to_all | solution.py:40
  549.0 12.1 %convolution_convert_fusion.1 = bf16[192,24,768]{2,1,0:T(8,128)(2,1)} fusion(f32[192,384]{1,0:T(8,128)S(1)} %bitcast.65, f32[192,384]{1,0:T(8,128)S(1)} %bitcast.66, pred[24]{0:T(512)(128)(4,1)S(1)} %add_compare_fusion, bf16[192,24,768]{2,1,0:T(8,128)(2,1)} %all_to_all.57, bf16[768,384]{1,0:T(8,128)(2,1)S(1)} %copy-done), kind=kOutput, calls=%fused_computation.9 | convolution fusion | flops 5444665344 | bytes 15335448 | tf_op jit(solution)/shard_map/kbj,yj->kby/dot_general | solution.py:46
  561.1 13.5 %copy.49 = bf16[192,24,768]{0,1,2:T(8,128)(2,1)} copy(bf16[192,24,768]{2,1,0:T(8,128)(2,1)} %convolution_convert_fusion.1) | data formatting | bytes 14155776 | tf_op jit(solution)/shard_map/convert_element_type | solution.py:46
  574.6 6.0 all-to-all-start.2
  580.6 19.8 %fusion.41 = bf16[1536,768,1]{1,0,2:T(8,128)(2,1)S(1)} fusion(s32[768]{0:T(1024)S(1)} %add_select_fusion.1, pred[768]{0:T(1024)(128)(4,1)S(1)} %iota_compare_fusion), kind=kLoop, calls=%fused_computation.21.clone.clone.1 | loop fusion | flops 14155776 | bytes 2363136 | tf_op jit(solution)/shard_map/kbx,nk->bxn/dot_general | solution.py:50
  600.4 185.1 %all-to-all-done.2 = bf16[192,24,768]{0,1,2:T(8,128)(2,1)} async-done(((bf16[192,24,768]{0,1,2:T(8,128)(2,1)}), bf16[192,24,768]{0,1,2:T(8,128)(2,1)}, u32[]{:S(2)}, u32[]{:S(2)}) %all-to-all-start.2) | async-done | bytes 7077920 | tf_op jit(solution)/shard_map/all_to_all | solution.py:49
  785.5 13.5 %copy.66 = bf16[192,24,4,192]{0,2,3,1:T(4,128)(2,1)} copy(bf16[192,24,4,192]{0,1,3,2:T(8,128)(2,1)} %bitcast.11) | data formatting | bytes 14155776 | tf_op jit(solution)/shard_map/all_to_all | solution.py:49
  799.0 16.6 %all_to_all.61 = bf16[768,24,192]{0,2,1:T(8,128)(2,1)} reshape(bf16[4,192,24,192]{1,0,3,2:T(4,128)(2,1)} %bitcast.62) | data formatting | bytes 14155776 | tf_op jit(solution)/shard_map/all_to_all | solution.py:49
  815.6 16.9 %convolution_convert_fusion = bf16[24,192,1536]{2,1,0:T(8,128)(2,1)} fusion(bf16[768,24,192]{0,2,1:T(8,128)(2,1)} %all_to_all.61, bf16[1536,768,1]{1,0,2:T(8,128)(2,1)S(1)} %fusion.41), kind=kOutput, calls=%fused_computation.2 | convolution fusion | flops 10878713856 | bytes 23592960 | tf_op jit(solution)/shard_map/kbx,nk->bxn/dot_general | solution.py:50
  832.5 26.0 %copy.51 = bf16[24,192,1536]{1,0,2:T(8,128)(2,1)} copy(bf16[24,192,1536]{2,1,0:T(8,128)(2,1)} %convolution_convert_fusion) | data formatting | bytes 28311552 | tf_op jit(solution)/shard_map/convert_element_type | solution.py:50
  858.6 7.3 all-to-all-start.3
  866.2 22.7 %reshape.40 = bf16[31,3,192,384]{3,2,0,1:T(8,128)(2,1)} reshape(bf16[31,3,1,1,73728]{4,0,3,2,1:T(8,128)(2,1)} %param.8) | data formatting | bytes 27426816 | tf_op jit(solution)/shard_map/reshape | solution.py:53
  889.0 182.5 %all-to-all-done.3 = bf16[24,192,1536]{1,0,2:T(8,128)(2,1)} async-done(((bf16[24,192,1536]{1,0,2:T(8,128)(2,1)}), bf16[24,192,1536]{1,0,2:T(8,128)(2,1)}, u32[]{:S(2)}, u32[]{:S(2)}) %all-to-all-start.3) | async-done | bytes 14155808 | tf_op jit(solution)/shard_map/all_to_all | solution.py:55
  1071.4 23.4 %copy.61 = bf16[24,192,4,384]{3,2,1,0:T(4,128)(2,1)} copy(bf16[24,192,4,384]{1,0,3,2:T(8,128)(2,1)} %bitcast.13) | data formatting | bytes 28311552 | tf_op jit(solution)/shard_map/all_to_all | solution.py:55
  1094.8 8.5 copy.53
  1103.9 4.1 multiply_reduce_fusion
  1108.3 1.5 reshape.41
  1109.8 41.3 %all-reduce.2.cloned.1.call-done = f32[3,1,1,73728]{3,0,2,1:T(4,128)} async-done(((f32[3,1,1,73728]{3,0,2,1:T(4,128)}), f32[3,1,1,73728]{3,0,2,1:T(4,128)}) %all-reduce.2.cloned.1.call-update) | async-done | bytes 884752 | tf_op jit(solution)/shard_map/psum | solution.py:63
  1151.0 3.1 copy.54
  (19 shorter events, 1.1 us)
Async XLA Ops:
  6.5 542.4 %copy-start = (bf16[768,384]{1,0:T(8,128)(2,1)S(1)}, bf16[768,384]{1,0:T(8,128)(2,1)}, u32[]{:S(2)}) copy-start(bf16[768,384]{1,0:T(8,128)(2,1)} %param.10) | copy-start | bytes 1769476
  96.8 162.6 %all-to-all-start = ((bf16[96,192,384]{2,1,0:T(8,128)(2,1)}), bf16[96,192,384]{2,1,0:T(8,128)(2,1)}, u32[]{:S(2)}, u32[]{:S(2)}) async-start(bf16[96,192,384]{2,1,0:T(8,128)(2,1)} %reshape.38), calls=%async_computation | async-start | bytes 28311552 | tf_op jit(solution)/shard_map/all_to_all | solution.py:36
  299.7 212.5 %all-to-all-start.1 = ((bf16[768,24,192]{2,1,0:T(8,128)(2,1)}), bf16[768,24,192]{2,1,0:T(8,128)(2,1)}, u32[]{:S(2)}, u32[]{:S(2)}) async-start(bf16[768,24,192]{2,1,0:T(8,128)(2,1)} %copy.47), calls=%async_computation.1 | async-start | bytes 18874368 | tf_op jit(solution)/shard_map/all_to_all | solution.py:40
  532.3 16.6 %copy-start.4 = (f32[384,192]{0,1:T(8,128)S(1)}, f32[384,192]{0,1:T(8,128)}, u32[]{:S(2)}) copy-start(f32[384,192]{0,1:T(8,128)} %param.11) | copy-start | bytes 884740
  532.3 16.6 %copy-start.5 = (f32[384,192]{0,1:T(8,128)S(1)}, f32[384,192]{0,1:T(8,128)}, u32[]{:S(2)}) copy-start(f32[384,192]{0,1:T(8,128)} %param.12) | copy-start | bytes 884740
  574.6 210.9 %all-to-all-start.2 = ((bf16[192,24,768]{0,1,2:T(8,128)(2,1)}), bf16[192,24,768]{0,1,2:T(8,128)(2,1)}, u32[]{:S(2)}, u32[]{:S(2)}) async-start(bf16[192,24,768]{0,1,2:T(8,128)(2,1)} %copy.49), calls=%async_computation.2 | async-start | bytes 18874368 | tf_op jit(solution)/shard_map/all_to_all | solution.py:49
  858.6 212.9 %all-to-all-start.3 = ((bf16[24,192,1536]{1,0,2:T(8,128)(2,1)}), bf16[24,192,1536]{1,0,2:T(8,128)(2,1)}, u32[]{:S(2)}, u32[]{:S(2)}) async-start(bf16[24,192,1536]{1,0,2:T(8,128)(2,1)} %copy.51), calls=%async_computation.3 | async-start | bytes 37748736 | tf_op jit(solution)/shard_map/all_to_all | solution.py:55
  865.9 23.0 %copy-start.3 = (f32[3]{0:T(128)S(1)}, f32[3]{0:T(128)}, u32[]{:S(2)}) copy-start(f32[3]{0:T(128)} %param.13) | copy-start | bytes 40
  865.9 285.1 %all-reduce.2.cloned.1.call-start = ((), (), s32[]{:S(2)}) async-start(), calls=%async_computation.4 | async-start | bytes 2359296 | tf_op jit(solution)/shard_map/psum | solution.py:63
  1094.8 9.2 copy-start.2
  1103.9 50.2 %copy-start.1 = (bf16[768,384]{1,0:T(8,128)(2,1)S(1)}, bf16[768,384]{1,0:T(8,128)(2,1)}, u32[]{:S(2)}) copy-start(bf16[768,384]{1,0:T(8,128)(2,1)} %param.10) | copy-start | bytes 1769476
Sparse Core Ops, SparseCore 0:
  1109.9 41.1 all-reduce.1
where the time goes:
time: 1170 us; the launch traced here: 1160 us
  waiting for transfers between devices  751 us (64%)
  local copies, waits for them, and re-layouts  272 us (23%)
  other arithmetic  52.6 us (4%)
  matrix products  45.4 us (4%)
  starting transfers between devices  26.8 us (2%)
  between operations  13.8 us (1%)
    all_to_all x1, waiting for transfers between devices, shards(): lax.all_to_all(waves, 'lat', split_axis=0, concat_axis=2, tiled=True)  206 us
    all_to_all x1, waiting for transfers between devices, shards(): lax.all_to_all(back, 'lat', split_axis=2, concat_axis=0, tiled=True)  185 us
    all_to_all x1, waiting for transfers between devices, shards(): lax.all_to_all(grid, 'lon', split_axis=2, concat_axis=0, tiled=True)  182 us
    all_to_all x1, waiting for transfers between devices, shards(): lax.all_to_all(fields, 'lon', split_axis=0, concat_axis=2, tiled=True)  136 us
    concatenate x1, local copies, waits for them, and re-layouts, shards(): jnp.concatenate([control, static_input[None]], 0)  48.5 us
    psum x1, waiting for transfers between devices, shards(): total = lax.psum(own, 'mem')  41.3 us
    all_to_all x2, local copies, waits for them, and re-layouts, shards(): lax.all_to_all(waves, 'lat', split_axis=0, concat_axis=2, tiled=True)  36.7 us
    all_to_all x2, local copies, waits for them, and re-layouts, shards(): lax.all_to_all(grid, 'lon', split_axis=2, concat_axis=0, tiled=True)  31.9 us
  transfers between devices with their start and end apart: 5, of which 5 were waited for; matrix products, arithmetic and copies ran while one was open for 5% of the time, Pallas kernels for 0%

commit v1 on v0

--- a/solution.py
+++ b/solution.py
@@ -2,6 +2,7 @@
 import jax.numpy as jnp
 from jax import lax
 from jax.sharding import PartitionSpec as P
+
 
 NLON = 1536
 NLAT = 768
@@ -20,7 +21,91 @@
     return values.astype(jnp.bfloat16)
 
 
-def shards(
+def swap(block, axis, step):
+    if step == 0:
+        return block
+    pairs = [(i, i ^ step) for i in range(lax.axis_size(axis))]
+    return lax.ppermute(block, axis, pairs)
+
+
+def pick(blocks, index):
+    return lax.dynamic_index_in_dim(blocks, index, 0, keepdims=False)
+
+
+def mul(spec, a, b):
+    return jnp.einsum(spec, a, b, preferred_element_type=jnp.float32)
+
+
+def by_fields(
+    control, perturbs, static_input, lat_basis, local_spectrum, static_spectrum, static_weight
+):
+    mem_dev, levels = control.shape[:2]
+    cell_count = control.shape[-1]
+    n_lat, n_lon = lax.axis_size("lat"), lax.axis_size("lon")
+    rows = NLAT // n_lat
+    cols = cell_count // rows
+    size = mem_dev + 1
+    part = size // n_lon
+    own_fields = part // n_lat
+    my_lon, my_lat = lax.axis_index("lon"), lax.axis_index("lat")
+    strips_basis = zonal_table().reshape(n_lon, cols, KLON)
+    near_strips = jnp.stack([pick(strips_basis, my_lon ^ e) for e in range(n_lon)])
+    near_zonal = near_strips.reshape(NLON, KLON)
+    bands_basis = lat_basis.reshape(n_lat, rows, -1)
+    near_bands = jnp.stack([pick(bands_basis, my_lat ^ d) for d in range(n_lat)])
+    near_merid = near_bands.reshape(NLAT, -1)
+    local_full = lax.all_gather(local_spectrum, "lat", axis=1, tiled=True)
+    static_full = lax.all_gather(static_spectrum, "lat", axis=1, tiled=True)
+    first = my_lon * part + my_lat * own_fields
+    is_static = first + jnp.arange(own_fields, dtype=jnp.int32) == mem_dev
+    spectrum = jnp.where(is_static[:, None, None], static_full[None], local_full[None])
+    first_mem = (lax.axis_index("mem") == 0).astype(jnp.float32)
+    increments = []
+    for level in range(levels):
+        fields = jnp.concatenate(
+            [control[:, level, 0, 0], static_input[level, 0, 0][None]], 0
+        ).reshape(n_lon, part, rows, cols)
+        strips = [pick(fields, my_lon ^ e) for e in range(n_lon)]
+        strips = [swap(strip, "lon", e) for e, strip in enumerate(strips)]
+        full_rows = jnp.concatenate(strips, -1)
+        waves = mul("fyn,nk->fyk", full_rows, near_zonal).astype(jnp.bfloat16)
+        if level == 0:
+            waves, perturbs = lax.optimization_barrier((waves, perturbs))
+        waves = waves.reshape(n_lat, own_fields, rows, KLON)
+        bands = [pick(waves, my_lat ^ d) for d in range(n_lat)]
+        bands = [swap(band, "lat", d) for d, band in enumerate(bands)]
+        columns = jnp.concatenate(bands, 1)
+        coef = mul("fyk,yj->fjk", columns, near_merid)
+        scaled = (coef * spectrum).astype(jnp.bfloat16)
+        back = [
+            mul("fjk,yj->fyk", scaled, near_bands[d]).astype(jnp.bfloat16)
+            for d in range(n_lat)
+        ]
+        back = [swap(block, "lat", d) for d, block in enumerate(back)]
+        back = jnp.stack(back)
+        rows_back = jnp.concatenate([pick(back, my_lat ^ d) for d in range(n_lat)], 0)
+        pert = perturbs[:, level, 0, 0]
+        pert = jnp.concatenate([pert, jnp.zeros_like(pert[:1])], 0)
+        pert = pert.reshape(n_lon, part, rows, cols)
+        ensemble = jnp.zeros((rows, cols), jnp.float32)
+        static_part = jnp.zeros((rows, cols), jnp.float32)
+        for e in range(n_lon):
+            grid = mul("fyk,nk->fyn", rows_back, near_strips[e]).astype(jnp.bfloat16)
+            filtered = swap(grid, "lon", e)
+            ensemble += mul("fyn,fyn->yn", pick(pert, my_lon ^ e), filtered)
+            static_here = (my_lon ^ e) == n_lon - 1
+            static_part += jnp.where(static_here, filtered[-1].astype(jnp.float32), 0.0)
+        weight = static_weight[level]
+        own = first_mem * weight * static_part + (1.0 - weight) * ensemble
+        if lax.axis_size("mem") == 2:
+            own += swap(own, "mem", 1)
+        else:
+            own = lax.psum(own, "mem")
+        increments.append(own)
+    return jnp.stack(increments).reshape(levels, 1, 1, cell_count)
+
+
+def by_waves(
     control, perturbs, static_input, lat_basis, local_spectrum, static_spectrum, static_weight
 ):
     mem_dev, levels = (control.shape[0], control.shape[1])
@@ -34,30 +119,22 @@
     first_mem = (lax.axis_index("mem") == 0).astype(jnp.float32)
     zonal = zonal_table()
     strips = lax.all_to_all(fields, "lon", split_axis=0, concat_axis=2, tiled=True)
-    waves = jnp.einsum("bxn,nk->kbx", strips, zonal, preferred_element_type=jnp.float32).astype(
-        jnp.bfloat16
-    )
+    waves = mul("bxn,nk->kbx", strips, zonal).astype(jnp.bfloat16)
     merid = lax.all_to_all(waves, "lat", split_axis=0, concat_axis=2, tiled=True)
-    coef = jnp.einsum("kby,yj->kbj", merid, lat_basis, preferred_element_type=jnp.float32)
+    coef = mul("kby,yj->kbj", merid, lat_basis)
     spectrum = jnp.where(
         is_static[None, :, None], static_spectrum.T[:, None, :], local_spectrum.T[:, None, :]
     )
     scaled = (coef * spectrum).astype(jnp.bfloat16)
-    back = jnp.einsum("kbj,yj->kby", scaled, lat_basis, preferred_element_type=jnp.float32).astype(
-        jnp.bfloat16
-    )
+    back = mul("kbj,yj->kby", scaled, lat_basis).astype(jnp.bfloat16)
     zonal_rows = lax.all_to_all(back, "lat", split_axis=2, concat_axis=0, tiled=True)
-    grid = jnp.einsum("kbx,nk->bxn", zonal_rows, zonal, preferred_element_type=jnp.float32).astype(
-        jnp.bfloat16
-    )
+    grid = mul("kbx,nk->bxn", zonal_rows, zonal).astype(jnp.bfloat16)
     pert_fields = perturbs.reshape(mem_dev, levels, lat_rows, lon_cols)
     weight = static_weight[:, None, None]
     filtered = lax.all_to_all(grid, "lon", split_axis=2, concat_axis=0, tiled=True).reshape(
         mem_dev + 1, levels, lat_rows, lon_cols
     )
-    ensemble = jnp.einsum(
-        "mlxn,mlxn->lxn", pert_fields, filtered[:mem_dev], preferred_element_type=jnp.float32
-    )
+    ensemble = mul("mlxn,mlxn->lxn", pert_fields, filtered[:mem_dev])
     static_part = filtered[mem_dev].astype(jnp.float32)
     own = first_mem * weight * static_part + (1.0 - weight) * ensemble
     total = lax.psum(own, "mem")
@@ -65,6 +142,12 @@
 
 
 def solution(mesh):
+    def shards(control, *rest):
+        group = lax.axis_size("lat") * lax.axis_size("lon")
+        uneven = (control.shape[0] + 1) % group or group & (group - 1)
+        body = by_waves if uneven else by_fields
+        return body(control, *rest)
+
     return jax.shard_map(
         shards,
         mesh=mesh,

time: 1170 us -> 632 us (0.54)
  waiting for transfers between devices: 751 us -> 293 us
  local copies, waits for them, and re-layouts: 272 us -> 51.5 us
  starting transfers between devices: 26.8 us -> 163 us
    all_to_all x4 -> x0, waiting for transfers between devices: 710 us -> none  [the longest x1 206 us: shards(): lax.all_to_all(waves, 'lat', split_axis=0, concat_axis=2, tiled=True)]
    ppermute x0 -> x39, waiting for transfers between devices: none -> 293 us  [swap(): return lax.ppermute(block, axis, pairs)]
    ppermute x0 -> x39, starting transfers between devices: none -> 163 us  [swap(): return lax.ppermute(block, axis, pairs)]
    all_to_all x7 -> x0, local copies, waits for them, and re-layouts: 109 us -> none  [the longest x2 36.7 us: shards(): lax.all_to_all(waves, 'lat', split_axis=0, concat_axis=2, tiled=True)]
    reshape x3 -> x0, local copies, waits for them, and re-layouts: 55.4 us -> none  [the longest x1 31.2 us: shards(): jnp.concatenate([control, static_input[None]], 0)]
    convert_element_type x3 -> x0, local copies, waits for them, and re-layouts: 52.9 us -> none  [the longest x1 26 us: shards(): jnp.einsum('kbx,nk->bxn', zonal_rows, zonal, preferred_element_type=jnp.f...]
    concatenate x1 -> x3, local copies, waits for them, and re-layouts: 48.5 us -> 0.92 us  [by_fields(): pert = jnp.concatenate([pert, jnp.zeros_like(pert[:1])], 0)]
    psum x1 -> x0, waiting for transfers between devices: 41.3 us -> none  [shards(): total = lax.psum(own, 'mem')]
  transfers between devices with their start and end apart: 5 -> 41, of which waited for: 5 -> 18; matrix products, arithmetic and copies ran while one was open for 5% -> 19% of each run, Pallas kernels for 0% -> 0%
where the time goes in v1:
time: 632 us; the launch traced here: 628 us
  waiting for transfers between devices  293 us (46%)
  starting transfers between devices  163 us (26%)
  other arithmetic  51.7 us (8%)
  local copies, waits for them, and re-layouts  51.5 us (8%)
  matrix products  50.9 us (8%)
  between operations  18.1 us (3%)
    ppermute x39, waiting for transfers between devices, swap(): return lax.ppermute(block, axis, pairs)  293 us
    ppermute x39, starting transfers between devices, swap(): return lax.ppermute(block, axis, pairs)  163 us
    dot_general x30, matrix products, mul(): return jnp.einsum(spec, a, b, preferred_element_type=jnp.float32)  50.9 us
    convert_element_type x1, other arithmetic, zonal_table(): return values.astype(jnp.bfloat16)  20.3 us
    unnamed x98, local copies, waits for them, and re-layouts  18.1 us
  transfers between devices with their start and end apart: 41, of which 18 were waited for; matrix products, arithmetic and copies ran while one was open for 19% of the time, Pallas kernels for 0%

profile of v1, /device:TPU:0, one launch (start us, length us, event | category | flops | bytes accessed | tf_op | source)
XLA Modules:
  0.0 628.4 jit_solution(4530152661289653392)
XLA Ops:
  9.0 10.9 %slice_bitcast_fusion.3 = (bf16[31,73728]{1,0:T(8,128)(2,1)}, bf16[31,73728]{1,0:T(8,128)(2,1)}, bf16[31,73728]{1,0:T(8,128)(2,1)}) fusion(bf16[31,3,1,1,73728]{4,0,3,2,1:T(8,128)(2,1)} %param.7), kind=kLoop, calls=%fused_computation.33 | loop fusion | bytes 27426816 | tf_op jit(solution)/shard_map/squeeze | solution.py:66
  20.0 7.6 %pad_maximum_fusion = (bf16[32,73728]{1,0:T(8,128)(2,1)S(1)}, bf16[32,73728]{1,0:T(8,128)(2,1)}) fusion(bf16[1,73728]{1,0:T(2,128)(2,1)S(1)} %get-tuple-element.68, bf16[31,73728]{1,0:T(8,128)(2,1)} %get-tuple-element.13, bf16[1,73728]{1,0:T(2,128)(2,1)S(1)} %get-tuple-element.67, bf16[31,73728]{1,0:T(8,128)(2,1)} %get-tuple-element.12), kind=kLoop, calls=%fused_computation.3 | loop fusion | flops 18874368 | bytes 18874368 | tf_op jit(solution)/shard_map/concatenate | solution.py:65
  44.0 4.7 constant_dynamic-slice_fusion.7
  62.4 20.3 %multiply_convert_fusion = bf16[4,384,768]{2,1,0:T(8,128)(2,1)S(1)} fusion(s32[768]{0:T(1024)S(1)} %add_select_fusion.1, s32[4,384]{1,0:T(4,128)S(1)} %multiply_add_fusion, pred[768]{0:T(1024)(128)(4,1)S(1)} %copy-done.37), kind=kLoop, calls=%fused_computation.35 | loop fusion | flops 14155776 | bytes 2369280 | tf_op jit(solution)/shard_map/convert_element_type | solution.py:21
  86.5 7.4 %fusion.62 = bf16[8,192,768]{2,1,0:T(8,128)(2,1)} fusion(bf16[1536,768,1]{1,0,2:T(8,128)(2,1)S(1)} %bitcast.343, bf16[8,192,384]{2,1,0:T(8,128)(2,1)} %collective-permute-done.2, bf16[8,192,384]{2,1,0:T(8,128)(2,1)} %collective-permute-done.1, bf16[8,192,384]{2,1,0:T(8,128)(2,1)} %collective-permute-done, bf16[8,192,384]{2,1,0:T(8,128)(2,1)S(1)} %bitcast.350), kind=kOutput, calls=%fused_computation.92 | convolution fusion | flops 3643932672 | bytes 9437184 | tf_op jit(solution)/shard_map/fyn,nk->fyk/dot_general | solution.py:36
  95.3 13.6 %collective-permute-done.28 = bf16[8,192,384]{2,1,0:T(8,128)(2,1)} collective-permute-done((bf16[8,192,384]{2,1,0:T(8,128)(2,1)}, bf16[8,192,384]{2,1,0:T(8,128)(2,1)}, u32[]{:S(2)}, u32[]{:S(2)}) %collective-permute-start.28) | collective-permute-done | bytes 1179680 | tf_op jit(solution)/shard_map/ppermute | solution.py:28
  109.8 25.5 %collective-permute-done.27 = bf16[8,192,384]{2,1,0:T(8,128)(2,1)} collective-permute-done((bf16[8,192,384]{2,1,0:T(8,128)(2,1)}, bf16[8,192,384]{2,1,0:T(8,128)(2,1)}, u32[]{:S(2)}, u32[]{:S(2)}) %collective-permute-start.27) | collective-permute-done | bytes 1179680 | tf_op jit(solution)/shard_map/ppermute | solution.py:28
  135.2 6.6 %fusion.56 = bf16[8,192,768]{2,1,0:T(8,128)(2,1)S(1)} fusion(bf16[1536,768,1]{1,0,2:T(8,128)(2,1)} %bitcast.344, bf16[8,192,384]{2,1,0:T(8,128)(2,1)} %collective-permute-done.28, bf16[8,192,384]{2,1,0:T(8,128)(2,1)} %collective-permute-done.27, bf16[8,192,384]{2,1,0:T(8,128)(2,1)} %collective-permute-done.26, bf16[8,192,384]{2,1,0:T(8,128)(2,1)S(1)} %bitcast.349), kind=kOutput, calls=%fused_computation.90 | convolution fusion | flops 3643932672 | bytes 9437184 | tf_op jit(solution)/shard_map/fyn,nk->fyk/dot_general | solution.py:36
  147.6 3.7 bitcast_convert_fusion.2
  154.9 4.6 collective-permute-done.15
  162.0 22.9 %collective-permute-done.14 = bf16[8,192,384]{2,1,0:T(8,128)(2,1)} collective-permute-done((bf16[8,192,384]{2,1,0:T(8,128)(2,1)}, bf16[8,192,384]{2,1,0:T(8,128)(2,1)}, u32[]{:S(2)}, u32[]{:S(2)}) %collective-permute-start.14) | collective-permute-done | bytes 1179680 | tf_op jit(solution)/shard_map/ppermute | solution.py:28
  185.0 5.5 fusion.59
  191.9 4.4 collective-permute-start.18
  199.4 3.8 bitcast_convert_fusion.10
  209.1 15.0 %collective-permute-done.30 = bf16[2,192,768]{2,1,0:T(8,128)(2,1)} collective-permute-done((bf16[2,192,768]{2,1,0:T(8,128)(2,1)}, bf16[2,192,768]{2,1,0:T(8,128)(2,1)}, u32[]{:S(2)}, u32[]{:S(2)}) %collective-permute-start.30) | collective-permute-done | bytes 589856 | tf_op jit(solution)/shard_map/ppermute | solution.py:28
  225.9 3.8 fusion.31
  231.7 30.9 %collective-permute-start.3 = (bf16[2,192,768]{2,1,0:T(8,128)(2,1)S(1)}, bf16[2,192,768]{2,1,0:T(8,128)(2,1)S(1)}, u32[]{:S(2)}, u32[]{:S(2)}) collective-permute-start(bf16[2,192,768]{2,1,0:T(8,128)(2,1)S(1)} %copy-done.34), channel_id=1, source_target_pairs={{0,4},{4,0},{8,12},{12,8},{1,5},{5,1},{9,13},{13,9},{2,6},{6,2},{1... | collective-permute-start | bytes 1769480 | tf_op jit(solution)/shard_map/ppermute | solution.py:28
  262.6 12.1 %collective-permute-done.17 = bf16[2,192,768]{2,1,0:T(8,128)(2,1)} collective-permute-done((bf16[2,192,768]{2,1,0:T(8,128)(2,1)}, bf16[2,192,768]{2,1,0:T(8,128)(2,1)}, u32[]{:S(2)}, u32[]{:S(2)}) %collective-permute-start.17) | collective-permute-done | bytes 589856 | tf_op jit(solution)/shard_map/ppermute | solution.py:28
  281.6 31.5 %collective-permute-start.32 = (bf16[2,192,768]{2,1,0:T(8,128)(2,1)S(1)}, bf16[2,192,768]{2,1,0:T(8,128)(2,1)S(1)}, u32[]{:S(2)}, u32[]{:S(2)}) collective-permute-start(bf16[2,192,768]{2,1,0:T(8,128)(2,1)S(1)} %fusion.80), channel_id=1, source_target_pairs={{0,4},{4,0},{8,12},{12,8},{1,5},{5,1},{9,13},{13,9},{2,6},{6,2},{1... | collective-permute-start | bytes 1769480 | tf_op jit(solution)/shard_map/ppermute | solution.py:28
  313.1 12.1 %collective-permute-done.4 = bf16[2,192,768]{2,1,0:T(8,128)(2,1)S(1)} collective-permute-done((bf16[2,192,768]{2,1,0:T(8,128)(2,1)}, bf16[2,192,768]{2,1,0:T(8,128)(2,1)S(1)}, u32[]{:S(2)}, u32[]{:S(2)}) %collective-permute-start.4) | collective-permute-done | bytes 589856 | tf_op jit(solution)/shard_map/ppermute | solution.py:28
  331.1 32.6 %collective-permute-start.19 = (bf16[2,192,768]{2,1,0:T(8,128)(2,1)S(1)}, bf16[2,192,768]{2,1,0:T(8,128)(2,1)S(1)}, u32[]{:S(2)}, u32[]{:S(2)}) collective-permute-start(bf16[2,192,768]{2,1,0:T(8,128)(2,1)S(1)} %fusion.76), channel_id=1, source_target_pairs={{0,4},{4,0},{8,12},{12,8},{1,5},{5,1},{9,13},{13,9},{2,6},{6,2},{1... | collective-permute-start | bytes 1769480 | tf_op jit(solution)/shard_map/ppermute | solution.py:28
  363.7 12.1 %collective-permute-done.33 = bf16[2,192,768]{2,1,0:T(8,128)(2,1)S(1)} collective-permute-done((bf16[2,192,768]{2,1,0:T(8,128)(2,1)S(1)}, bf16[2,192,768]{2,1,0:T(8,128)(2,1)S(1)}, u32[]{:S(2)}, u32[]{:S(2)}) %collective-permute-start.33) | collective-permute-done | bytes 589856 | tf_op jit(solution)/shard_map/ppermute | solution.py:28
  384.0 30.4 %collective-permute-start.6 = (bf16[2,192,768]{2,1,0:T(8,128)(2,1)S(1)}, bf16[2,192,768]{2,1,0:T(8,128)(2,1)S(1)}, u32[]{:S(2)}, u32[]{:S(2)}) collective-permute-start(bf16[2,192,768]{2,1,0:T(8,128)(2,1)S(1)} %fusion.72), channel_id=1, source_target_pairs={{0,4},{4,0},{8,12},{12,8},{1,5},{5,1},{9,13},{13,9},{2,6},{6,2},{1... | collective-permute-start | bytes 1769480 | tf_op jit(solution)/shard_map/ppermute | solution.py:28
  414.3 12.1 %collective-permute-done.20 = bf16[2,192,768]{2,1,0:T(8,128)(2,1)S(1)} collective-permute-done((bf16[2,192,768]{2,1,0:T(8,128)(2,1)S(1)}, bf16[2,192,768]{2,1,0:T(8,128)(2,1)S(1)}, u32[]{:S(2)}, u32[]{:S(2)}) %collective-permute-start.20) | collective-permute-done | bytes 589856 | tf_op jit(solution)/shard_map/ppermute | solution.py:28
  429.8 21.0 %collective-permute-done.7 = bf16[2,192,768]{2,1,0:T(8,128)(2,1)S(1)} collective-permute-done((bf16[2,192,768]{2,1,0:T(8,128)(2,1)S(1)}, bf16[2,192,768]{2,1,0:T(8,128)(2,1)S(1)}, u32[]{:S(2)}, u32[]{:S(2)}) %collective-permute-start.7) | collective-permute-done | bytes 589856 | tf_op jit(solution)/shard_map/ppermute | solution.py:28
  466.5 16.1 %collective-permute-done.37 = bf16[8,192,384]{2,1,0:T(8,128)(2,1)S(1)} collective-permute-done((bf16[8,192,384]{2,1,0:T(8,128)(2,1)S(1)}, bf16[8,192,384]{2,1,0:T(8,128)(2,1)S(1)}, u32[]{:S(2)}, u32[]{:S(2)}) %collective-permute-start.37) | collective-permute-done | bytes 1179680 | tf_op jit(solution)/shard_map/ppermute | solution.py:28
  483.2 24.8 %collective-permute-done.36 = bf16[8,192,384]{2,1,0:T(8,128)(2,1)S(1)} collective-permute-done((bf16[8,192,384]{2,1,0:T(8,128)(2,1)S(1)}, bf16[8,192,384]{2,1,0:T(8,128)(2,1)S(1)}, u32[]{:S(2)}, u32[]{:S(2)}) %collective-permute-start.36) | collective-permute-done | bytes 1179680 | tf_op jit(solution)/shard_map/ppermute | solution.py:28
  510.9 22.3 %collective-permute-done.24 = bf16[8,192,384]{2,1,0:T(8,128)(2,1)S(1)} collective-permute-done((bf16[8,192,384]{2,1,0:T(8,128)(2,1)S(1)}, bf16[8,192,384]{2,1,0:T(8,128)(2,1)S(1)}, u32[]{:S(2)}, u32[]{:S(2)}) %collective-permute-start.24) | collective-permute-done | bytes 1179680 | tf_op jit(solution)/shard_map/ppermute | solution.py:28
  533.8 24.8 %collective-permute-done.23 = bf16[8,192,384]{2,1,0:T(8,128)(2,1)S(1)} collective-permute-done((bf16[8,192,384]{2,1,0:T(8,128)(2,1)S(1)}, bf16[8,192,384]{2,1,0:T(8,128)(2,1)S(1)}, u32[]{:S(2)}, u32[]{:S(2)}) %collective-permute-start.23) | collective-permute-done | bytes 1179680 | tf_op jit(solution)/shard_map/ppermute | solution.py:28
  561.9 21.9 %collective-permute-done.11 = bf16[8,192,384]{2,1,0:T(8,128)(2,1)S(1)} collective-permute-done((bf16[8,192,384]{2,1,0:T(8,128)(2,1)S(1)}, bf16[8,192,384]{2,1,0:T(8,128)(2,1)S(1)}, u32[]{:S(2)}, u32[]{:S(2)}) %collective-permute-start.11) | collective-permute-done | bytes 1179680 | tf_op jit(solution)/shard_map/ppermute | solution.py:28
  584.2 24.9 %collective-permute-done.10 = bf16[8,192,384]{2,1,0:T(8,128)(2,1)S(1)} collective-permute-done((bf16[8,192,384]{2,1,0:T(8,128)(2,1)S(1)}, bf16[8,192,384]{2,1,0:T(8,128)(2,1)S(1)}, u32[]{:S(2)}, u32[]{:S(2)}) %collective-permute-start.10) | collective-permute-done | bytes 1179680 | tf_op jit(solution)/shard_map/ppermute | solution.py:28
  612.5 6.8 %collective-permute-done.12 = f32[192,384]{1,0:T(8,128)S(1)} collective-permute-done((f32[192,384]{1,0:T(8,128)S(1)}, f32[192,384]{1,0:T(8,128)S(1)}, u32[]{:S(2)}, u32[]{:S(2)}) %collective-permute-start.12) | collective-permute-done | bytes 294944 | tf_op jit(solution)/shard_map/ppermute | solution.py:28
  (235 shorter events, 113.6 us)
Async XLA Ops:
  6.5 196.7 %all-gather.5.cloned.1.call-start = ((), (), s32[]{:S(2)}) async-start(), calls=%async_computation.1 | async-start | bytes 1474560 | tf_op jit(solution)/shard_map/all_gather | solution.py:57
  29.3 55.0 %collective-permute-start.2 = (bf16[8,192,384]{2,1,0:T(8,128)(2,1)}, bf16[8,192,384]{2,1,0:T(8,128)(2,1)}, u32[]{:S(2)}, u32[]{:S(2)}) collective-permute-start(bf16[8,192,384]{2,1,0:T(8,128)(2,1)} %bitcast.330), channel_id=1, source_target_pairs={{0,3},{1,2},{2,1},{3,0},{4,7},{5,6},{6,5},{7,4},{8,11},{9,10},{10,... | collective-permute-start | bytes 3538952 | tf_op jit(solution)/shard_map/ppermute | solution.py:28
  34.8 171.2 %all-gather.3.cloned.1.call-start = ((), (), s32[]{:S(2)}) async-start(), calls=%async_computation | async-start | bytes 1474560 | tf_op jit(solution)/shard_map/all_gather | solution.py:58
  39.6 69.3 %collective-permute-start.28 = (bf16[8,192,384]{2,1,0:T(8,128)(2,1)}, bf16[8,192,384]{2,1,0:T(8,128)(2,1)}, u32[]{:S(2)}, u32[]{:S(2)}) collective-permute-start(bf16[8,192,384]{2,1,0:T(8,128)(2,1)} %bitcast.322), channel_id=1, source_target_pairs={{0,3},{1,2},{2,1},{3,0},{4,7},{5,6},{6,5},{7,4},{8,11},{9,10},{10,... | collective-permute-start | bytes 3538952 | tf_op jit(solution)/shard_map/ppermute | solution.py:28
  42.3 93.0 %collective-permute-start.27 = (bf16[8,192,384]{2,1,0:T(8,128)(2,1)}, bf16[8,192,384]{2,1,0:T(8,128)(2,1)}, u32[]{:S(2)}, u32[]{:S(2)}) collective-permute-start(bf16[8,192,384]{2,1,0:T(8,128)(2,1)} %bitcast.323), channel_id=1, source_target_pairs={{0,2},{1,3},{2,0},{3,1},{4,6},{5,7},{6,4},{7,5},{8,10},{9,11},{10,... | collective-permute-start | bytes 3538952 | tf_op jit(solution)/shard_map/ppermute | solution.py:28
  84.7 74.8 %collective-permute-start.15 = (bf16[8,192,384]{2,1,0:T(8,128)(2,1)}, bf16[8,192,384]{2,1,0:T(8,128)(2,1)}, u32[]{:S(2)}, u32[]{:S(2)}) collective-permute-start(bf16[8,192,384]{2,1,0:T(8,128)(2,1)} %bitcast.326), channel_id=1, source_target_pairs={{0,3},{1,2},{2,1},{3,0},{4,7},{5,6},{6,5},{7,4},{8,11},{9,10},{10,... | collective-permute-start | bytes 3538952 | tf_op jit(solution)/shard_map/ppermute | solution.py:28
  85.9 99.0 %collective-permute-start.14 = (bf16[8,192,384]{2,1,0:T(8,128)(2,1)}, bf16[8,192,384]{2,1,0:T(8,128)(2,1)}, u32[]{:S(2)}, u32[]{:S(2)}) collective-permute-start(bf16[8,192,384]{2,1,0:T(8,128)(2,1)} %bitcast.327), channel_id=1, source_target_pairs={{0,2},{1,3},{2,0},{3,1},{4,6},{5,7},{6,4},{7,5},{8,10},{9,11},{10,... | collective-permute-start | bytes 3538952 | tf_op jit(solution)/shard_map/ppermute | solution.py:28
  108.9 76.0 %collective-permute-start.13 = (bf16[8,192,384]{2,1,0:T(8,128)(2,1)}, bf16[8,192,384]{2,1,0:T(8,128)(2,1)S(1)}, u32[]{:S(2)}, u32[]{:S(2)}) collective-permute-start(bf16[8,192,384]{2,1,0:T(8,128)(2,1)} %bitcast.328), channel_id=1, source_target_pairs={{0,1},{1,0},{2,3},{3,2},{4,5},{5,4},{6,7},{7,6},{8,9},{9,8},{10,11... | collective-permute-start | bytes 3538952 | tf_op jit(solution)/shard_map/ppermute | solution.py:28
  143.4 65.2 %collective-permute-start.31 = (bf16[2,192,768]{2,1,0:T(8,128)(2,1)}, bf16[2,192,768]{2,1,0:T(8,128)(2,1)}, u32[]{:S(2)}, u32[]{:S(2)}) collective-permute-start(bf16[2,192,768]{2,1,0:T(8,128)(2,1)} %get-tuple-element.60), channel_id=1, source_target_pairs={{0,12},{4,8},{8,4},{12,0},{1,13},{5,9},{9,5},{13,1},{2,14},{6,10},... | collective-permute-start | bytes 1769480 | tf_op jit(solution)/shard_map/ppermute | solution.py:28
  147.0 77.1 %collective-permute-start.30 = (bf16[2,192,768]{2,1,0:T(8,128)(2,1)}, bf16[2,192,768]{2,1,0:T(8,128)(2,1)}, u32[]{:S(2)}, u32[]{:S(2)}) collective-permute-start(bf16[2,192,768]{2,1,0:T(8,128)(2,1)} %get-tuple-element.61), channel_id=1, source_target_pairs={{0,8},{4,12},{8,0},{12,4},{1,9},{5,13},{9,1},{13,5},{2,10},{6,14},... | collective-permute-start | bytes 1769480 | tf_op jit(solution)/shard_map/ppermute | solution.py:28
  159.5 66.4 %collective-permute-start.29 = (bf16[2,192,768]{2,1,0:T(8,128)(2,1)}, bf16[2,192,768]{2,1,0:T(8,128)(2,1)}, u32[]{:S(2)}, u32[]{:S(2)}) collective-permute-start(bf16[2,192,768]{2,1,0:T(8,128)(2,1)} %get-tuple-element.62), channel_id=1, source_target_pairs={{0,4},{4,0},{8,12},{12,8},{1,5},{5,1},{9,13},{13,9},{2,6},{6,2},{1... | collective-permute-start | bytes 1769480 | tf_op jit(solution)/shard_map/ppermute | solution.py:28
  196.3 78.4 %collective-permute-start.17 = (bf16[2,192,768]{2,1,0:T(8,128)(2,1)}, bf16[2,192,768]{2,1,0:T(8,128)(2,1)}, u32[]{:S(2)}, u32[]{:S(2)}) collective-permute-start(bf16[2,192,768]{2,1,0:T(8,128)(2,1)} %get-tuple-element.53), channel_id=1, source_target_pairs={{0,8},{4,12},{8,0},{12,4},{1,9},{5,13},{9,1},{13,5},{2,10},{6,14},... | collective-permute-start | bytes 1769480 | tf_op jit(solution)/shard_map/ppermute | solution.py:28
  208.6 66.2 %collective-permute-start.16 = (bf16[2,192,768]{2,1,0:T(8,128)(2,1)}, bf16[2,192,768]{2,1,0:T(8,128)(2,1)S(1)}, u32[]{:S(2)}, u32[]{:S(2)}) collective-permute-start(bf16[2,192,768]{2,1,0:T(8,128)(2,1)} %get-tuple-element.54), channel_id=1, source_target_pairs={{0,4},{4,0},{8,12},{12,8},{1,5},{5,1},{9,13},{13,9},{2,6},{6,2},{1... | collective-permute-start | bytes 1769480 | tf_op jit(solution)/shard_map/ppermute | solution.py:28
  224.1 57.5 %collective-permute-start.5 = (bf16[2,192,768]{2,1,0:T(8,128)(2,1)}, bf16[2,192,768]{2,1,0:T(8,128)(2,1)S(1)}, u32[]{:S(2)}, u32[]{:S(2)}) collective-permute-start(bf16[2,192,768]{2,1,0:T(8,128)(2,1)} %get-tuple-element.44), channel_id=1, source_target_pairs={{0,12},{4,8},{8,4},{12,0},{1,13},{5,9},{9,5},{13,1},{2,14},{6,10},... | collective-permute-start | bytes 1769480 | tf_op jit(solution)/shard_map/ppermute | solution.py:28
  225.9 99.4 %collective-permute-start.4 = (bf16[2,192,768]{2,1,0:T(8,128)(2,1)}, bf16[2,192,768]{2,1,0:T(8,128)(2,1)S(1)}, u32[]{:S(2)}, u32[]{:S(2)}) collective-permute-start(bf16[2,192,768]{2,1,0:T(8,128)(2,1)} %get-tuple-element.45), channel_id=1, source_target_pairs={{0,8},{4,12},{8,0},{12,4},{1,9},{5,13},{9,1},{13,5},{2,10},{6,14},... | collective-permute-start | bytes 1769480 | tf_op jit(solution)/shard_map/ppermute | solution.py:28
  231.7 93.5 %collective-permute-start.3 = (bf16[2,192,768]{2,1,0:T(8,128)(2,1)S(1)}, bf16[2,192,768]{2,1,0:T(8,128)(2,1)S(1)}, u32[]{:S(2)}, u32[]{:S(2)}) collective-permute-start(bf16[2,192,768]{2,1,0:T(8,128)(2,1)S(1)} %copy-done.34), channel_id=1, source_target_pairs={{0,4},{4,0},{8,12},{12,8},{1,5},{5,1},{9,13},{13,9},{2,6},{6,2},{1... | collective-permute-start | bytes 1769480 | tf_op jit(solution)/shard_map/ppermute | solution.py:28
  280.6 95.2 %collective-permute-start.33 = (bf16[2,192,768]{2,1,0:T(8,128)(2,1)S(1)}, bf16[2,192,768]{2,1,0:T(8,128)(2,1)S(1)}, u32[]{:S(2)}, u32[]{:S(2)}) collective-permute-start(bf16[2,192,768]{2,1,0:T(8,128)(2,1)S(1)} %fusion.81), channel_id=1, source_target_pairs={{0,8},{4,12},{8,0},{12,4},{1,9},{5,13},{9,1},{13,5},{2,10},{6,14},... | collective-permute-start | bytes 1769480 | tf_op jit(solution)/shard_map/ppermute | solution.py:28
  281.6 96.7 %collective-permute-start.32 = (bf16[2,192,768]{2,1,0:T(8,128)(2,1)S(1)}, bf16[2,192,768]{2,1,0:T(8,128)(2,1)S(1)}, u32[]{:S(2)}, u32[]{:S(2)}) collective-permute-start(bf16[2,192,768]{2,1,0:T(8,128)(2,1)S(1)} %fusion.80), channel_id=1, source_target_pairs={{0,4},{4,0},{8,12},{12,8},{1,5},{5,1},{9,13},{13,9},{2,6},{6,2},{1... | collective-permute-start | bytes 1769480 | tf_op jit(solution)/shard_map/ppermute | solution.py:28
  327.6 56.3 %collective-permute-start.21 = (bf16[2,192,768]{2,1,0:T(8,128)(2,1)S(1)}, bf16[2,192,768]{2,1,0:T(8,128)(2,1)S(1)}, u32[]{:S(2)}, u32[]{:S(2)}) collective-permute-start(bf16[2,192,768]{2,1,0:T(8,128)(2,1)S(1)} %fusion.78), channel_id=1, source_target_pairs={{0,12},{4,8},{8,4},{12,0},{1,13},{5,9},{9,5},{13,1},{2,14},{6,10},... | collective-permute-start | bytes 1769480 | tf_op jit(solution)/shard_map/ppermute | solution.py:28
  330.1 96.3 %collective-permute-start.20 = (bf16[2,192,768]{2,1,0:T(8,128)(2,1)S(1)}, bf16[2,192,768]{2,1,0:T(8,128)(2,1)S(1)}, u32[]{:S(2)}, u32[]{:S(2)}) collective-permute-start(bf16[2,192,768]{2,1,0:T(8,128)(2,1)S(1)} %fusion.77), channel_id=1, source_target_pairs={{0,8},{4,12},{8,0},{12,4},{1,9},{5,13},{9,1},{13,5},{2,10},{6,14},... | collective-permute-start | bytes 1769480 | tf_op jit(solution)/shard_map/ppermute | solution.py:28
  331.1 95.3 %collective-permute-start.19 = (bf16[2,192,768]{2,1,0:T(8,128)(2,1)S(1)}, bf16[2,192,768]{2,1,0:T(8,128)(2,1)S(1)}, u32[]{:S(2)}, u32[]{:S(2)}) collective-permute-start(bf16[2,192,768]{2,1,0:T(8,128)(2,1)S(1)} %fusion.76), channel_id=1, source_target_pairs={{0,4},{4,0},{8,12},{12,8},{1,5},{5,1},{9,13},{13,9},{2,6},{6,2},{1... | collective-permute-start | bytes 1769480 | tf_op jit(solution)/shard_map/ppermute | solution.py:28
  375.9 53.9 %collective-permute-start.8 = (bf16[2,192,768]{2,1,0:T(8,128)(2,1)S(1)}, bf16[2,192,768]{2,1,0:T(8,128)(2,1)S(1)}, u32[]{:S(2)}, u32[]{:S(2)}) collective-permute-start(bf16[2,192,768]{2,1,0:T(8,128)(2,1)S(1)} %fusion.74), channel_id=1, source_target_pairs={{0,12},{4,8},{8,4},{12,0},{1,13},{5,9},{9,5},{13,1},{2,14},{6,10},... | collective-permute-start | bytes 1769480 | tf_op jit(solution)/shard_map/ppermute | solution.py:28
  378.3 72.5 %collective-permute-start.7 = (bf16[2,192,768]{2,1,0:T(8,128)(2,1)S(1)}, bf16[2,192,768]{2,1,0:T(8,128)(2,1)S(1)}, u32[]{:S(2)}, u32[]{:S(2)}) collective-permute-start(bf16[2,192,768]{2,1,0:T(8,128)(2,1)S(1)} %fusion.73), channel_id=1, source_target_pairs={{0,8},{4,12},{8,0},{12,4},{1,9},{5,13},{9,1},{13,5},{2,10},{6,14},... | collective-permute-start | bytes 1769480 | tf_op jit(solution)/shard_map/ppermute | solution.py:28
  384.0 66.8 %collective-permute-start.6 = (bf16[2,192,768]{2,1,0:T(8,128)(2,1)S(1)}, bf16[2,192,768]{2,1,0:T(8,128)(2,1)S(1)}, u32[]{:S(2)}, u32[]{:S(2)}) collective-permute-start(bf16[2,192,768]{2,1,0:T(8,128)(2,1)S(1)} %fusion.72), channel_id=1, source_target_pairs={{0,4},{4,0},{8,12},{12,8},{1,5},{5,1},{9,13},{13,9},{2,6},{6,2},{1... | collective-permute-start | bytes 1769480 | tf_op jit(solution)/shard_map/ppermute | solution.py:28
  454.8 53.3 %collective-permute-start.36 = (bf16[8,192,384]{2,1,0:T(8,128)(2,1)S(1)}, bf16[8,192,384]{2,1,0:T(8,128)(2,1)S(1)}, u32[]{:S(2)}, u32[]{:S(2)}) collective-permute-start(bf16[8,192,384]{2,1,0:T(8,128)(2,1)S(1)} %convolution_convert_fusion.1), channel_id=1, source_target_pairs={{0,2},{1,3},{2,0},{3,1},{4,6},{5,7},{6,4},{7,5},{8,10},{9,11},{10,... | collective-permute-start | bytes 3538952 | tf_op jit(solution)/shard_map/ppermute | solution.py:28
  458.1 75.1 %collective-permute-start.24 = (bf16[8,192,384]{2,1,0:T(8,128)(2,1)S(1)}, bf16[8,192,384]{2,1,0:T(8,128)(2,1)S(1)}, u32[]{:S(2)}, u32[]{:S(2)}) collective-permute-start(bf16[8,192,384]{2,1,0:T(8,128)(2,1)S(1)} %convolution_convert_fusion.4), channel_id=1, source_target_pairs={{0,3},{1,2},{2,1},{3,0},{4,7},{5,6},{6,5},{7,4},{8,11},{9,10},{10,... | collective-permute-start | bytes 3538952 | tf_op jit(solution)/shard_map/ppermute | solution.py:28
  459.3 99.3 %collective-permute-start.23 = (bf16[8,192,384]{2,1,0:T(8,128)(2,1)S(1)}, bf16[8,192,384]{2,1,0:T(8,128)(2,1)S(1)}, u32[]{:S(2)}, u32[]{:S(2)}) collective-permute-start(bf16[8,192,384]{2,1,0:T(8,128)(2,1)S(1)} %convolution_convert_fusion.5), channel_id=1, source_target_pairs={{0,2},{1,3},{2,0},{3,1},{4,6},{5,7},{6,4},{7,5},{8,10},{9,11},{10,... | collective-permute-start | bytes 3538952 | tf_op jit(solution)/shard_map/ppermute | solution.py:28
  482.6 78.0 %collective-permute-start.22 = (bf16[8,192,384]{2,1,0:T(8,128)(2,1)S(1)}, bf16[8,192,384]{2,1,0:T(8,128)(2,1)S(1)}, u32[]{:S(2)}, u32[]{:S(2)}) collective-permute-start(bf16[8,192,384]{2,1,0:T(8,128)(2,1)S(1)} %convolution_convert_fusion.6), channel_id=1, source_target_pairs={{0,1},{1,0},{2,3},{3,2},{4,5},{5,4},{6,7},{7,6},{8,9},{9,8},{10,11... | collective-permute-start | bytes 3538952 | tf_op jit(solution)/shard_map/ppermute | solution.py:28
  508.0 75.7 %collective-permute-start.11 = (bf16[8,192,384]{2,1,0:T(8,128)(2,1)S(1)}, bf16[8,192,384]{2,1,0:T(8,128)(2,1)S(1)}, u32[]{:S(2)}, u32[]{:S(2)}) collective-permute-start(bf16[8,192,384]{2,1,0:T(8,128)(2,1)S(1)} %convolution_convert_fusion.8), channel_id=1, source_target_pairs={{0,3},{1,2},{2,1},{3,0},{4,7},{5,6},{6,5},{7,4},{8,11},{9,10},{10,... | collective-permute-start | bytes 3538952 | tf_op jit(solution)/shard_map/ppermute | solution.py:28
  509.4 99.7 %collective-permute-start.10 = (bf16[8,192,384]{2,1,0:T(8,128)(2,1)S(1)}, bf16[8,192,384]{2,1,0:T(8,128)(2,1)S(1)}, u32[]{:S(2)}, u32[]{:S(2)}) collective-permute-start(bf16[8,192,384]{2,1,0:T(8,128)(2,1)S(1)} %convolution_convert_fusion.9), channel_id=1, source_target_pairs={{0,2},{1,3},{2,0},{3,1},{4,6},{5,7},{6,4},{7,5},{8,10},{9,11},{10,... | collective-permute-start | bytes 3538952 | tf_op jit(solution)/shard_map/ppermute | solution.py:28
  533.2 76.4 %collective-permute-start.9 = (bf16[8,192,384]{2,1,0:T(8,128)(2,1)S(1)}, bf16[8,192,384]{2,1,0:T(8,128)(2,1)S(1)}, u32[]{:S(2)}, u32[]{:S(2)}) collective-permute-start(bf16[8,192,384]{2,1,0:T(8,128)(2,1)S(1)} %convolution_convert_fusion.10), channel_id=1, source_target_pairs={{0,1},{1,0},{2,3},{3,2},{4,5},{5,4},{6,7},{7,6},{8,9},{9,8},{10,11... | collective-permute-start | bytes 3538952 | tf_op jit(solution)/shard_map/ppermute | solution.py:28
  558.6 53.2 %collective-permute-start.38 = (f32[192,384]{1,0:T(8,128)S(1)}, f32[192,384]{1,0:T(8,128)S(1)}, u32[]{:S(2)}, u32[]{:S(2)}) collective-permute-start(f32[192,384]{1,0:T(8,128)S(1)} %bitcast_add_fusion), channel_id=1, source_target_pairs={{0,16},{16,0},{1,17},{17,1},{2,18},{18,2},{3,19},{19,3},{4,20},{20... | collective-permute-start | bytes 884744 | tf_op jit(solution)/shard_map/ppermute | solution.py:28
  (52 other events, 1079.5 us)
Sparse Core Ops, SparseCore 0:
  34.9 31.7 all-gather.4
  68.3 29.4 all-gather.2
